TPU v7x, 32 devices: a whole 2x2x4 slice. The times are simulated.
32 devices in a mesh: dp: 8 (over z, x), mp: 4 (over y, core).
Axes of the slice: x: 2, y: 2, z: 4, core: 2. Of those that a mesh axis runs over, the one named last changes fastest.
Arguments:
- stats: float32 [4, 64, 256, 256], P('mp', 'dp'), may hold values from -1 to 1, as said below
- prev_roots: float32 [4, 64, 256, 256], P('mp', 'dp'), may hold values from -1 to 2, as said below
- counts: int32 [4, 8], replicated, may hold values from 1 to 8, as said below
- grads: bfloat16 [4, 64, 256, 1024], P(None, 'dp', None, 'mp'), may hold values from -6 to 6
Outputs:
- precond: bfloat16 [4, 64, 256, 1024], P(None, 'dp', None, 'mp')
Inputs may be any that keep to these rules, and one draw needn't show every extreme that they name: Each model shard's live blocks are the first count slots of each of its devices; every count is 1 to 8, 8 is reached on some device, and the counts of one model shard sum to at most 32, which some model shard reaches. `stats`: every block is symmetric positive definite. `prev_roots`: every block is symmetric.
All inputs are finite; a program needn't handle non-finite values.
Results may differ from a plain program's by a relative error of at most 0.0052.
Values may be sent and summed in bfloat16 or wider, within the bound.
A program may use at most 128 MiB of HBM per device.

v0:
```python
import functools

import jax
import jax.numpy as jnp
from jax import lax
from jax.experimental import pallas as pl
from jax.experimental.pallas import tpu as pltpu
from jax.sharding import PartitionSpec as P

NEWTON = 2
PIECES = 1
VMEM_BYTES = 67043328 - 65536
MESH = pl.DeviceIdType.MESH


def dot(left, right):
    return jnp.dot(left.astype(jnp.bfloat16), right.astype(jnp.bfloat16), preferred_element_type=jnp.float32)


def shifted_square(part):
    return 2.0 * part + dot(part, part)


def newton_root(statistic, initial):
    size = initial.shape[-1]
    rows = lax.broadcasted_iota(jnp.int32, (size, size), 0)
    columns = lax.broadcasted_iota(jnp.int32, (size, size), 1)
    identity = jnp.where(rows == columns, 1.0, 0.0).astype(jnp.float32)
    moment = statistic + dot(shifted_square(shifted_square(initial - identity)), statistic)
    estimate = initial
    for iteration in range(NEWTON):
        change = 0.25 * (identity - moment)
        estimate = estimate + dot(estimate, change)
        if iteration + 1 < NEWTON:
            moment = moment + dot(shifted_square(shifted_square(change)), moment)
    return estimate


def kernel(members, count_table, stats, starts, grads, out, counts, count_sem, a_buf, x_buf, g_buf, roots,
           a_sem, x_sem, g_sem, y_send, y_recv, p_send, p_recv, f_send, f_recv):
    me = lax.axis_index("mp")
    data = lax.axis_index("dp")
    slots = stats.shape[1]
    chips = members // 2
    core = lax.rem(me, 2)
    chip = me // 2
    partner = me + 1 - 2 * core

    def peer(offset, which):
        return lax.rem(chip + offset, chips) * 2 + which

    def a_copy(slot):
        return pltpu.make_async_copy(stats.at[0, slot], a_buf.at[slot], a_sem.at[slot])

    def x_copy(slot):
        return pltpu.make_async_copy(starts.at[0, slot], x_buf.at[slot], x_sem.at[slot])

    def g_copy(owner):
        return pltpu.make_async_copy(grads.at[owner], g_buf.at[owner], g_sem.at[owner])

    def send(block, target, send_sem, recv_sem):
        return pltpu.make_async_remote_copy(
            src_ref=block, dst_ref=block, send_sem=send_sem, recv_sem=recv_sem,
            device_id={"mp": target}, device_id_type=MESH)

    height = roots.shape[2] // PIECES

    def strip(piece):
        return pl.ds(pl.multiple_of(piece * height, height), height)

    def y_copy(owner, offset, slot, piece):
        at = offset - 1, slot, piece
        return send(roots.at[owner, slot, strip(piece)], peer(offset, core), y_send.at[at], y_recv.at[at])

    def p_copy(owner, slot):
        return send(roots.at[owner, slot], partner, p_send.at[slot], p_recv.at[slot])

    def f_copy(owner, offset, slot, piece):
        at = offset - 1, slot, piece
        return send(roots.at[owner, slot, strip(piece)], partner, f_send.at[at], f_recv.at[at])

    count_copy = pltpu.make_async_copy(count_table, counts, count_sem)
    x_copy(0).start()
    a_copy(0).start()
    count_copy.start()

    barrier = pltpu.get_barrier_semaphore()
    pl.semaphore_signal(barrier, inc=1, device_id={"mp": partner}, device_id_type=MESH)
    for offset in range(1, chips):
        pl.semaphore_signal(barrier, inc=1, device_id={"mp": peer(offset, core)}, device_id_type=MESH)

    count_copy.wait()
    live_count = counts[me, data]

    def compute(slot):
        root = newton_root(a_buf[slot], x_buf[slot])
        live = jnp.full(root.shape, slot, jnp.int32) < live_count
        roots[me, slot] = jnp.where(live, root, 0.0).astype(jnp.bfloat16)

    def launch(slot):
        for piece in range(PIECES):
            for offset in range(1, chips):
                y_copy(me, offset, slot, piece).start()
        p_copy(me, slot).start()

    x_copy(0).wait()
    a_copy(0).wait()
    for slot in range(1, slots):
        x_copy(slot).start()
        a_copy(slot).start()
    for owner in range(members):
        g_copy(owner).start()
    compute(0)
    pl.semaphore_wait(barrier, chips)
    launch(0)

    @pl.loop(1, slots)
    def _(slot):
        x_copy(slot).wait()
        a_copy(slot).wait()
        compute(slot)
        launch(slot)

    for owner in range(members):
        g_copy(owner).wait()

    def apply(owner, slot):
        out[owner, slot] = dot(roots[owner, slot], g_buf[owner, slot]).astype(out.dtype)

    @pl.loop(0, slots)
    def _(slot):
        apply(me, slot)
        p_copy(partner, slot).wait_recv()
        apply(partner, slot)

    def apply_strip(owner, slot, piece):
        part = strip(piece)
        out[owner, slot, part] = dot(roots[owner, slot, part], g_buf[owner, slot]).astype(out.dtype)

    def arrive(count):
        slot, piece = count // PIECES, lax.rem(count, PIECES)
        for offset in range(1, chips):
            owner = peer(chips - offset, core)
            y_copy(owner, offset, slot, piece).wait_recv()
            f_copy(owner, offset, slot, piece).start()
            apply_strip(owner, slot, piece)

    def passed(count):
        slot, piece = count // PIECES, lax.rem(count, PIECES)
        for offset in range(1, chips):
            owner = peer(chips - offset, 1 - core)
            f_copy(owner, offset, slot, piece).wait_recv()
            apply_strip(owner, slot, piece)

    arrive(jnp.int32(0))

    @pl.loop(1, slots * PIECES)
    def _(count):
        arrive(count)
        passed(count - 1)

    passed(jnp.int32(slots * PIECES - 1))

    @pl.loop(0, slots)
    def _(slot):
        p_copy(me, slot).wait_send()
        for piece in range(PIECES):
            for offset in range(1, chips):
                y_copy(me, offset, slot, piece).wait_send()
                f_copy(peer(chips - offset, core), offset, slot, piece).wait_send()


def local(members, stats, prev_roots, counts, grads):
    slots, size = stats.shape[1], stats.shape[2]
    chips = members // 2
    block = (slots, size, size)
    out_bytes = grads.size * grads.dtype.itemsize
    return pl.pallas_call(
        functools.partial(kernel, members),
        out_shape=pltpu.VMEM(grads.shape, grads.dtype),
        in_specs=[pl.BlockSpec(memory_space=pltpu.HBM)] * 4,
        out_specs=pl.BlockSpec(memory_space=pltpu.VMEM),
        scratch_shapes=[
            pltpu.SMEM(counts.shape, counts.dtype),
            pltpu.SemaphoreType.DMA,
            pltpu.VMEM(block, jnp.float32),
            pltpu.VMEM(block, jnp.float32),
            pltpu.VMEM(grads.shape, grads.dtype),
            pltpu.VMEM((members,) + block, jnp.bfloat16),
            pltpu.SemaphoreType.DMA((slots,)),
            pltpu.SemaphoreType.DMA((slots,)),
            pltpu.SemaphoreType.DMA((members,)),
            pltpu.SemaphoreType.DMA((chips - 1, slots, PIECES)),
            pltpu.SemaphoreType.DMA((chips - 1, slots, PIECES)),
            pltpu.SemaphoreType.DMA((slots,)),
            pltpu.SemaphoreType.DMA((slots,)),
            pltpu.SemaphoreType.DMA((chips - 1, slots, PIECES)),
            pltpu.SemaphoreType.DMA((chips - 1, slots, PIECES)),
        ],
        compiler_params=pltpu.CompilerParams(
            collective_id=0, has_side_effects=True, vmem_limit_bytes=VMEM_BYTES - out_bytes),
    )(counts, stats, prev_roots, grads)


def solution(mesh):
    return jax.shard_map(
        functools.partial(local, mesh.shape["mp"]),
        mesh=mesh,
        in_specs=(
            P("mp", "dp", None, None),
            P("mp", "dp", None, None),
            P(),
            P(None, "dp", None, "mp"),
        ),
        out_specs=P(None, "dp", None, "mp"),
        check_vma=False,
    )
```

profile of v0, /device:TPU:0, one launch (start us, length us, event | category | flops | bytes accessed | tf_op | source)
XLA Modules:
  0.0 32.0 jit_solution(8942792139735262943)
XLA Ops:
  0.0 30.0 %shard_map.46 = bf16[4,8,256,256]{3,2,1,0:T(8,128)(2,1)S(1)} custom-call(s32[4,8]{1,0:T(4,128)} %count_table.1, f32[1,8,256,256]{3,2,1,0:T(8,128)} %stats.1, f32[1,8,256,256]{3,2,1,0:T(8,128)} %starts.1, bf16[4,8,256,256]{3,2,1,0:T(8,128)(2,1)} %grads.1), custom_call_target="tpu_custom_call" | custom-call | tf_op jit(solution)/shard_map/pallas_call | solution.py:178
  30.0 2.0 %copy.6 = bf16[4,8,256,256]{3,2,1,0:T(8,128)(2,1)} copy(bf16[4,8,256,256]{3,2,1,0:T(8,128)(2,1)S(1)} %shard_map.46) | data formatting | bytes 8388608
where the time goes:
time: 32.3 us; the launch traced here: 32 us
  Pallas kernels  30 us (93%)
  local copies, waits for them, and re-layouts  2.02 us (6%)
    pallas_call x1, Pallas kernels, local(): pl.pallas_call(functools.partial(kernel, members), out_shape=pltpu.VMEM(g...  30 us
    unnamed x1, local copies, waits for them, and re-layouts  2.02 us

commit v1 on v0

v1 whole, which is shorter than its diff:
```python
import functools

import jax
import jax.numpy as jnp
from jax import lax
from jax.experimental import pallas as pl
from jax.experimental.pallas import tpu as pltpu
from jax.sharding import PartitionSpec as P

VMEM_BYTES = 67043328 - 65536
MESH = pl.DeviceIdType.MESH
RELAYS = 3
WINDOW = 3


def dot(left, right):
    return jnp.dot(left.astype(jnp.bfloat16), right.astype(jnp.bfloat16), preferred_element_type=jnp.float32)


def shifted_squares(parts):
    return [2.0 * part + dot(part, part) for part in parts]


def newton_roots(statistics, initials):
    size = initials[0].shape[-1]
    rows = lax.broadcasted_iota(jnp.int32, (size, size), 0)
    columns = lax.broadcasted_iota(jnp.int32, (size, size), 1)
    identity = jnp.where(rows == columns, 1.0, 0.0).astype(jnp.float32)
    fourths = shifted_squares(shifted_squares([initial - identity for initial in initials]))
    moments = [statistic + dot(fourth, statistic) for fourth, statistic in zip(fourths, statistics)]
    changes = [0.25 * (identity - moment) for moment in moments]
    estimates = [initial + dot(initial, change) for initial, change in zip(initials, changes)]
    fourths = shifted_squares(shifted_squares(changes))
    moments = [moment + dot(fourth, moment) for fourth, moment in zip(fourths, moments)]
    changes = [0.25 * (identity - moment) for moment in moments]
    return [estimate + dot(estimate, change) for estimate, change in zip(estimates, changes)]


def packed_at(index, first, second, slots):
    both = jnp.minimum(first, second)
    paired = index < 2 * both
    slot = jnp.where(paired, lax.div(index, 2), index - both)
    core = jnp.where(paired, lax.rem(index, 2), jnp.where(first > second, 0, 1))
    return core, jnp.clip(slot, 0, slots - 1)


def neighbour_of(data):
    return data + 1 - 2 * lax.rem(data, 2)


def relayed_block(number):
    return number % 2, 1 + number // 2


class Load:
    def __init__(self, counts, chip, data, positions):
        self.first, self.second = counts[2 * chip, data], counts[2 * chip + 1, data]
        self.excess = jnp.maximum(self.first + self.second - positions, 0)


def choosing_kernel(sizes, relays, counts, choice):
    members, workers = counts.shape
    need = jnp.int32(0)
    for chip in range(members // 2):
        for data in range(0, workers, 2):
            pair = [counts[2 * chip, at] + counts[2 * chip + 1, at] for at in (data, data + 1)]
            need = jnp.maximum(need, lax.div(pair[0] + pair[1] + 1, 2))
            need = jnp.maximum(need, jnp.maximum(*pair) - relays)
    choice[0] = sum((need > size).astype(jnp.int32) for size in sizes[:-1])


def kernel(members, positions, relays, window, count_table, stats, starts, grads, near, far, counts, count_sem,
           a_buf, x_buf, g_buf, pool, staged, landed, relayed, returned, a_sem, x_sem, g_sem, y_send, y_recv, p_send, p_recv,
           f_send, f_recv, r_send, r_recv, b_send, b_recv, h_send, h_recv):
    me = lax.axis_index("mp")
    data = lax.axis_index("dp")
    slots, size = stats.shape[1], stats.shape[2]
    chips = members // 2
    core = lax.rem(me, 2)
    chip = me // 2
    other = 1 - core
    partner = 2 * chip + other
    beside = neighbour_of(data)
    half = size // 2
    group = 4

    def rows_of(which):
        return pl.ds(pl.multiple_of(which * half, half), half)

    def peer(offset):
        return lax.rem(chip + offset, chips) * 2 + core

    def source_of(offset):
        return lax.rem(chip + chips - offset, chips)

    def a_copy(slot):
        return pltpu.make_async_copy(stats.at[0, slot], a_buf.at[slot], a_sem.at[slot])

    def x_copy(slot):
        return pltpu.make_async_copy(starts.at[0, slot], x_buf.at[slot], x_sem.at[slot])

    def g_copy(owner):
        return pltpu.make_async_copy(grads.at[owner], g_buf.at[owner], g_sem.at[owner])

    def send(source, place, target, send_sem, recv_sem):
        return pltpu.make_async_remote_copy(
            src_ref=source, dst_ref=place, send_sem=send_sem, recv_sem=recv_sem,
            device_id=target, device_id_type=MESH)

    def p_copy(which, slot):
        block = pool.at[which, slot]
        return send(block, block, {"mp": partner}, p_send.at[slot], p_recv.at[slot])

    def first_copy(offset):
        return send(pool.at[core, 0], landed.at[offset - 1, core], {"mp": peer(offset)},
                    y_send.at[offset - 1, 0], y_recv.at[offset - 1, 0])

    def first_forward(offset, which):
        block = landed.at[offset - 1, which]
        return send(block, block, {"mp": partner}, f_send.at[offset - 1, 0], f_recv.at[offset - 1, 0])

    def y_copy(offset, position):
        return send(staged.at[position - 2], landed.at[offset - 1, position, rows_of(core)], {"mp": peer(offset)},
                    y_send.at[offset - 1, position - 1], y_recv.at[offset - 1, position - 1])

    def forward(offset, position, which):
        block = landed.at[offset - 1, position, rows_of(which)]
        return send(block, block, {"mp": partner}, f_send.at[offset - 1, position - 1], f_recv.at[offset - 1, position - 1])

    def relay_copy(number, which):
        at_core, at_slot = relayed_block(number)
        return send(pool.at[at_core, at_slot, rows_of(which)], relayed.at[number], {"dp": beside, "mp": 2 * chip + which},
                    r_send.at[number, which], r_recv.at[number])

    def back_copy(offset, number):
        return send(landed.at[offset - 1, window + number, rows_of(core)], returned.at[offset - 1, number, rows_of(core)],
                    {"dp": beside, "mp": me}, b_send.at[offset - 1, number], b_recv.at[offset - 1, number])

    def back_forward(offset, number, which):
        block = returned.at[offset - 1, number, rows_of(which)]
        return send(block, block, {"mp": partner}, h_send.at[offset - 1, number], h_recv.at[offset - 1, number])

    count_copy = pltpu.make_async_copy(count_table, counts, count_sem)
    for slot in range(group):
        x_copy(slot).start()
    for slot in range(group):
        a_copy(slot).start()
    count_copy.start()

    barrier = pltpu.get_barrier_semaphore()
    pl.semaphore_signal(barrier, inc=1, device_id={"mp": partner}, device_id_type=MESH)
    for offset in range(1, chips):
        pl.semaphore_signal(barrier, inc=1, device_id={"mp": peer(offset)}, device_id_type=MESH)
    for which in range(2):
        pl.semaphore_signal(barrier, inc=1, device_id={"dp": beside, "mp": 2 * chip + which}, device_id_type=MESH)
    greeted = chips + 2

    count_copy.wait()
    live_count = counts[me, data]
    mine, theirs = Load(counts, chip, data, positions), Load(counts, chip, beside, positions)

    for slot in range(group):
        x_copy(slot).wait()
        a_copy(slot).wait()
    for slot in range(group, slots):
        x_copy(slot).start()
        a_copy(slot).start()
    for owner in range(members):
        g_copy(owner).start()

    @pl.loop(0, slots // group)
    def _(turn):
        batch = [turn * group + at for at in range(group)]

        @pl.when(turn > 0)
        def _():
            for slot in batch:
                x_copy(slot).wait()
                a_copy(slot).wait()

        found = newton_roots([a_buf[slot] for slot in batch], [x_buf[slot] for slot in batch])
        for slot, root in zip(batch, found):
            live = jnp.full(root.shape, slot, jnp.int32) < live_count
            pool[core, slot] = jnp.where(live, root, 0.0).astype(jnp.bfloat16)

        @pl.when(turn == 0)
        def _():
            pl.semaphore_wait(barrier, greeted)
            for offset in range(1, chips):
                first_copy(offset).start()
            for number in range(relays):
                @pl.when(core == relayed_block(number)[0])
                def _():
                    for which in range(2):
                        relay_copy(number, which).start()

        for slot in batch:
            p_copy(core, slot).start()

    def launch(position, excess, taken=None):
        at_core, at_slot = packed_at(position + excess, mine.first, mine.second, slots)
        value = pool[at_core, at_slot, rows_of(core)]
        if taken is not None:
            value = lax.select_n(taken < theirs.excess, value, relayed[taken])
        staged[position - 2] = value
        for offset in range(1, chips):
            y_copy(offset, position).start()

    def near_apply(which):
        @pl.loop(0, slots // group)
        def _(turn):
            for at in range(group):
                slot = turn * group + at
                near[which, slot] = dot(pool[which, slot], g_buf[2 * chip + which, slot]).astype(near.dtype)

    for owner in range(members):
        g_copy(owner).wait()
    near_apply(core)

    @pl.loop(0, slots)
    def _(slot):
        p_copy(other, slot).wait_recv()

    @pl.loop(2, window)
    def _(position):
        launch(position, mine.excess)

    for number in range(relays):
        relay_copy(number, core).wait_recv()
        launch(window + number, mine.excess - theirs.excess, number)

    @pl.loop(window + relays, positions)
    def _(position):
        launch(position, mine.excess - theirs.excess)

    near_apply(other)
    last = far.shape[1] - 1
    for at in range(chips - 1):
        far[at, last] = jnp.zeros(far.shape[2:], far.dtype)

    loads = {offset: (Load(counts, source_of(offset), data, positions), Load(counts, source_of(offset), beside, positions))
             for offset in range(1, chips)}

    def arrive(kind, number):
        for offset in range(1, chips):
            if kind == "first":
                first_copy(offset).wait_recv()
                first_forward(offset, core).start()
            elif kind == "position":
                y_copy(offset, number).wait_recv()
                forward(offset, number, core).start()
                if window <= number < window + relays:
                    back_copy(offset, number - window).start()
            else:
                back_copy(offset, number).wait_recv()
                back_forward(offset, number, core).start()

    def apply(offset, kind, number):
        source = source_of(offset)
        at = offset - 1
        if kind == "first":
            first_forward(offset, other).wait_recv()
            for which in range(2):
                far[at, which] = dot(landed[at, which], g_buf[2 * source + which, 0]).astype(far.dtype)
        elif kind == "position":
            forward(offset, number, other).wait_recv()
            own, side = loads[offset]
            index = number + own.excess
            if number >= window:
                index = index - side.excess
            at_core, at_slot = packed_at(index, own.first, own.second, slots)
            far[at, number] = dot(landed[at, number], g_buf[2 * source + at_core, at_slot]).astype(far.dtype)
        else:
            back_forward(offset, number, other).wait_recv()
            at_core, at_slot = relayed_block(number)
            far[at, positions + number] = dot(returned[at, number], g_buf[2 * source + at_core, at_slot]).astype(far.dtype)

    events = [(2.0, "first", 0)]
    events += [(position + 1.0, "position", position) for position in range(2, positions)]
    events += [(window + number + 3.6, "back", number) for number in range(relays)]
    events = [event[1:] for event in sorted(events)]
    arrive(*events[0])
    for before, now in zip(events, events[1:]):
        arrive(*now)
        for offset in range(1, chips):
            apply(offset, *before)
    for offset in range(1, chips):
        apply(offset, *events[-1])

    @pl.loop(0, slots)
    def _(slot):
        p_copy(core, slot).wait_send()

    for number in range(relays):
        @pl.when(core == relayed_block(number)[0])
        def _():
            for which in range(2):
                relay_copy(number, which).wait_send()

    for offset in range(1, chips):
        first_copy(offset).wait_send()
        first_forward(offset, core).wait_send()
        for number in range(relays):
            back_copy(offset, number).wait_send()
            back_forward(offset, number, core).wait_send()

        @pl.loop(2, positions)
        def _(position):
            y_copy(offset, position).wait_send()
            forward(offset, position, core).wait_send()


def placing_kernel(members, positions, relays, window, count_table, near, far, out, counts, count_sem, near_sem, far_sem):
    me = lax.axis_index("mp")
    data = lax.axis_index("dp")
    chips = members // 2
    chip = me // 2
    slots = near.shape[1]
    count_copy = pltpu.make_async_copy(count_table, counts, count_sem)
    count_copy.start()

    def near_copy(which):
        return pltpu.make_async_copy(near.at[which], out.at[2 * chip + which], near_sem.at[which])

    for which in range(2):
        near_copy(which).start()
    count_copy.wait()
    copies = []
    for offset in range(1, chips):
        source = lax.rem(chip + chips - offset, chips)
        own, side = Load(counts, source, data, positions), Load(counts, source, neighbour_of(data), positions)
        both = jnp.minimum(own.first, own.second)
        for which in range(2):
            for slot in range(slots):
                index = jnp.where(slot < both, 2 * slot + which, slot + both)
                kept = jnp.where(index < 2, index, index - own.excess)
                place = jnp.where(kept < window, kept, kept + side.excess)
                handed = (index >= 2) & (index < 2 + own.excess)
                place = jnp.where(handed, positions + index - 2, place)
                place = jnp.where(slot < (own.first, own.second)[which], place, far.shape[1] - 1)
                copies.append(pltpu.make_async_copy(
                    far.at[offset - 1, place], out.at[2 * source + which, slot], far_sem.at[offset - 1, which, slot]))
                copies[-1].start()
    for which in range(2):
        near_copy(which).wait()
    for copy in copies:
        copy.wait()


def exchange(members, number, positions, relays, window, stats, prev_roots, counts, grads):
    slots, size = stats.shape[1], stats.shape[2]
    chips = members // 2
    square = (size, size)
    near = (2, slots) + square
    far = (chips - 1, positions + relays + 1) + square
    kept = grads.dtype.itemsize * size * size * (near[0] * near[1] + far[0] * far[1])
    semaphores = pltpu.SemaphoreType.DMA
    steps, backs = (chips - 1, positions - 1), (chips - 1, relays)
    near, far = pl.pallas_call(
        functools.partial(kernel, members, positions, relays, window),
        out_shape=(pltpu.VMEM(near, grads.dtype), pltpu.VMEM(far, grads.dtype)),
        in_specs=[pl.BlockSpec(memory_space=pltpu.HBM)] * 4,
        out_specs=(pl.BlockSpec(memory_space=pltpu.VMEM), pl.BlockSpec(memory_space=pltpu.VMEM)),
        scratch_shapes=[
            pltpu.SMEM(counts.shape, counts.dtype),
            semaphores,
            pltpu.VMEM((slots,) + square, jnp.float32),
            pltpu.VMEM((slots,) + square, jnp.float32),
            pltpu.VMEM(grads.shape, grads.dtype),
            pltpu.VMEM((2, slots) + square, jnp.bfloat16),
            pltpu.VMEM((positions - 2, size // 2, size), jnp.bfloat16),
            pltpu.VMEM((chips - 1, positions) + square, jnp.bfloat16),
            pltpu.VMEM((relays, size // 2, size), jnp.bfloat16),
            pltpu.VMEM((chips - 1, relays) + square, jnp.bfloat16),
            semaphores((slots,)),
            semaphores((slots,)),
            semaphores((members,)),
            semaphores(steps),
            semaphores(steps),
            semaphores((slots,)),
            semaphores((slots,)),
            semaphores(steps),
            semaphores(steps),
            semaphores((relays, 2)),
            semaphores((relays,)),
            semaphores(backs),
            semaphores(backs),
            semaphores(backs),
            semaphores(backs),
        ],
        compiler_params=pltpu.CompilerParams(
            collective_id=number, has_side_effects=True, vmem_limit_bytes=VMEM_BYTES - kept),
    )(counts, stats, prev_roots, grads)
    return pl.pallas_call(
        functools.partial(placing_kernel, members, positions, relays, window),
        out_shape=pltpu.HBM(grads.shape, grads.dtype),
        in_specs=[
            pl.BlockSpec(memory_space=pltpu.HBM),
            pl.BlockSpec(memory_space=pltpu.VMEM),
            pl.BlockSpec(memory_space=pltpu.VMEM),
        ],
        out_specs=pl.BlockSpec(memory_space=pltpu.HBM),
        scratch_shapes=[
            pltpu.SMEM(counts.shape, counts.dtype),
            semaphores,
            semaphores((2,)),
            semaphores((chips - 1, 2, slots)),
        ],
        compiler_params=pltpu.CompilerParams(vmem_limit_bytes=1 << 20),
    )(counts, near, far)


def local(members, stats, prev_roots, counts, grads):
    slots = stats.shape[1]
    sizes = list(range(slots + 1, slots + 5)) + [2 * slots]
    choice = pl.pallas_call(
        functools.partial(choosing_kernel, sizes, RELAYS),
        out_shape=jax.ShapeDtypeStruct((1,), jnp.int32),
        in_specs=[pl.BlockSpec(memory_space=pltpu.SMEM)],
        out_specs=pl.BlockSpec(memory_space=pltpu.SMEM),
    )(counts)
    branches = [functools.partial(exchange, members, number, size, RELAYS, WINDOW) for number, size in enumerate(sizes)]
    return lax.switch(choice[0], branches, stats, prev_roots, counts, grads)


def solution(mesh):
    return jax.shard_map(
        functools.partial(local, mesh.shape["mp"]),
        mesh=mesh,
        in_specs=(
            P("mp", "dp", None, None),
            P("mp", "dp", None, None),
            P(),
            P(None, "dp", None, "mp"),
        ),
        out_specs=P(None, "dp", None, "mp"),
        check_vma=False,
    )
```

time: 32.3 us -> 27.9 us (0.86)
  Pallas kernels: 30 us -> 26.6 us
  local copies, waits for them, and re-layouts: 2.02 us -> 0.01 us
  between operations: 0.01 us -> 0.84 us
    pallas_call x1 -> x3, Pallas kernels: 30 us -> 26.6 us  [the longest x1 23.2 us: exchange(): pl.pallas_call(functools.partial(kernel, members, positions, relays, wind...]
    unnamed x1 -> x0, local copies, waits for them, and re-layouts: 2.02 us -> none
where the time goes in v1:
time: 27.9 us; the launch traced here: 27.7 us
  Pallas kernels  26.6 us (95%)
  between operations  0.84 us (3%)
  loops' own time  0.28 us (1%)
    pallas_call x1, Pallas kernels, exchange(): pl.pallas_call(functools.partial(kernel, members, positions, relays, wind...  23.2 us
    pallas_call x1, Pallas kernels, exchange(): pl.pallas_call(functools.partial(placing_kernel, members, positions, rela...  2.17 us
    pallas_call x1, Pallas kernels, local(): pl.pallas_call(functools.partial(choosing_kernel, sizes, RELAYS), out_sha...  1.26 us

profile of v1, /device:TPU:0, one launch (start us, length us, event | category | flops | bytes accessed | tf_op | source)
XLA Modules:
  0.0 27.7 jit_solution(16662698683185186109)
XLA Ops:
  0.0 1.3 %shard_map.66 = s32[1]{0:T(128)} custom-call(s32[4,8]{1,0:T(4,128)} %counts.1), custom_call_target="tpu_custom_call" | custom-call | tf_op jit(solution)/shard_map/pallas_call | solution.py:416
  1.9 25.6 %conditional.1 = (bf16[4,8,256,256]{3,2,1,0:T(8,128)(2,1)}) conditional(s32[]{:T(128)} %bitcast, (s32[4,8]{1,0:T(4,128)}, f32[1,8,256,256]{3,2,1,0:T(8,128)}, f32[1,8,256,256]{3,2,1,0:T(8,128)}, bf16[4,8,256,256]{3,2,1,0:T(8,128)(2,1)}) %tuple.20, (s32[4,8]{1,0:T(4,128)}, f32[1,8,256,256]{3,2,1,0:T(8,128)}, ...), branch_computations={%region_0.0_spmd, %region_1.0_spmd, %region_2.0_spmd, %region_3.0_... | conditional | bytes 548 | solution.py:423
  1.9 0.0 copy-start
  1.9 23.2 %branch_0_fun.2 = (bf16[2,8,256,256]{3,2,1,0:T(8,128)(2,1)S(1)}, bf16[1,13,256,256]{3,2,1,0:T(8,128)(2,1)S(1)}) custom-call(s32[4,8]{1,0:T(4,128)} %get-tuple-element.44.count_table, f32[1,8,256,256]{3,2,1,0:T(8,128)} %get-tuple-element.97.stats, f32[1,8,256,256]{3,2,1,0:T(8,128)} %get-tuple-element.102.starts, bf16[4,8,256,256]{3,2,1,0:T(8,128)(2,1)} %get-tuple-element.107.grads), custom_call_target="tpu_custom_call" | custom-call | tf_op jit(solution)/shard_map/cond/branch_0_fun/pallas_call | solution.py:359
  25.1 0.0 copy-done
  25.1 2.2 %branch_0_fun.3 = bf16[4,8,256,256]{3,2,1,0:T(8,128)(2,1)} custom-call(s32[4,8]{1,0:T(4,128)S(1)} %copy-done, bf16[2,8,256,256]{3,2,1,0:T(8,128)(2,1)S(1)} %get-tuple-element.55.near, bf16[1,13,256,256]{3,2,1,0:T(8,128)(2,1)S(1)} %get-tuple-element.56.far), custom_call_target="tpu_custom_call" | custom-call | tf_op jit(solution)/shard_map/cond/branch_0_fun/pallas_call | solution.py:394
Async XLA Ops:
  1.9 23.2 %copy-start = (s32[4,8]{1,0:T(4,128)S(1)}, s32[4,8]{1,0:T(4,128)}, u32[]{:S(2)}) copy-start(s32[4,8]{1,0:T(4,128)} %get-tuple-element.44.count_table) | copy-start | bytes 388 | tf_op jit(solution)/shard_map/cond
